TPU v7x, 256 devices: a whole 4x4x8 slice. The times are simulated.
256 devices in a mesh: expert: 8 (over y, core), shard: 32 (over z, x).
Axes of the slice: x: 4, y: 4, z: 8, core: 2. Of those that a mesh axis runs over, the one named last changes fastest.
Arguments:
- master_gate: float32 [128, 2048, 768], P('expert', 'shard'), may hold values from -0.125 to 0.125
- second_gate: bfloat16 [128, 2048, 768], P('expert', 'shard'), may hold values from -0.0625 to 0.0625
- master_up: float32 [128, 2048, 768], P('expert', 'shard'), may hold values from -0.125 to 0.125
- second_up: bfloat16 [128, 2048, 768], P('expert', 'shard'), may hold values from -0.0625 to 0.0625
- router_weight: float32 [2048, 128], P('shard', 'expert'), may hold values from -0.125 to 0.125
- router_gain: float32 [2048], P('shard'), may hold values from 0.25 to 1.75
Outputs:
- final_gate: bfloat16 [128, 768, 2048], P('expert', 'shard')
- final_up: bfloat16 [128, 768, 2048], P('expert', 'shard')
- serve_router: bfloat16 [2048, 128], replicated
All inputs are finite; a program needn't handle non-finite values.
Results may differ from a plain program's by a relative error of at most 0.001.
Values may be sent and summed in bfloat16 or wider, within the bound.
A program may use at most 64 MiB of HBM per device.

v0:
```python
import jax
import jax.numpy as jnp
from jax import lax
from jax.sharding import Mesh
from jax.sharding import PartitionSpec as P

EXPERT = ("expert_0", "expert_1")


def laid_out(parts, dim):
    shape = list(parts.shape[1:])
    shape[dim] *= parts.shape[0]
    return jnp.moveaxis(parts, 0, dim).reshape(shape)


def copy_for_each(x, axis):
    copies = jnp.broadcast_to(x, (lax.axis_size(axis), *x.shape))
    return lax.all_to_all(copies, axis, split_axis=0, concat_axis=0, tiled=True)


def gathered_copies(x, axis, dim):
    return laid_out(copy_for_each(x, axis), dim)


def edges_of(length, count):
    turn = length // count
    if turn >= 8:
        turn -= turn % 8
    return [turn * k for k in range(1, count)]


def gather_in_order(x, axes, turns):
    parts = x
    for k in turns:
        parts = lax.all_gather(parts, axes[k])
    done = turns[::-1]
    back = [done.index(k) for k in range(len(axes))]
    parts = parts.transpose(*back, *range(len(axes), parts.ndim))
    return parts.reshape(-1, *x.shape)


def gather_all_axes(x, axes, dim):
    numbers = list(range(len(axes)))[::-1]
    cut = x.shape.index(max(x.shape[:-1] or x.shape))
    edges = [0, *edges_of(x.shape[cut], len(axes)), x.shape[cut]]
    gathered = []
    for k, (start, end) in enumerate(zip(edges, edges[1:])):
        if end > start:
            section = lax.slice_in_dim(x, start, end, axis=cut)
            gathered.append(gather_in_order(section, axes, numbers[k:] + numbers[:k]))
    return laid_out(jnp.concatenate(gathered, axis=cut + 1), dim)


def shards(master_gate, second_gate, master_up, second_up, router_weight, router_gain):
    merged_gate = master_gate + second_gate.astype(jnp.float32)
    merged_up = master_up + second_up.astype(jnp.float32)
    narrow_gate, narrow_up = (merged_gate.astype(jnp.bfloat16), merged_up.astype(jnp.bfloat16))
    final_gate, final_up = (
        lax.all_to_all(narrow_gate, "shard", split_axis=2, concat_axis=1, tiled=True),
        lax.all_to_all(narrow_up, "shard", split_axis=2, concat_axis=1, tiled=True),
    )
    final_gate = jnp.transpose(final_gate, (0, 2, 1))
    final_up = jnp.transpose(final_up, (0, 2, 1))
    part_router = (router_weight * router_gain[:, None]).astype(jnp.bfloat16)
    row_router = gathered_copies(part_router, "shard", 0)
    serve_router = gather_all_axes(row_router, EXPERT, 1)
    return (final_gate, final_up, serve_router)


def solution(mesh):
    split = Mesh(mesh.devices.reshape(4, 2, mesh.shape["shard"]), ("expert_0", "expert_1", "shard"))
    in_specs = (
        P(EXPERT, "shard", None),
        P(EXPERT, "shard", None),
        P(EXPERT, "shard", None),
        P(EXPERT, "shard", None),
        P("shard", EXPERT),
        P("shard"),
    )
    out_specs = (P(EXPERT, "shard", None), P(EXPERT, "shard", None), P())
    return jax.shard_map(
        shards, mesh=split, in_specs=in_specs, out_specs=out_specs, check_vma=False
    )
```

profile of v0, /device:TPU:6, one launch (start us, length us, event | category | flops | bytes accessed | tf_op | source)
XLA Modules:
  0.0 138.5 jit_solution(3208780866263310215)
XLA Ops:
  0.6 0.7 multiply_convert_fusion
  1.4 0.8 reshape.31
  2.1 11.6 %all-to-all-start.2 = ((bf16[32,2,512]{2,1,0:T(2,128)(2,1)}), bf16[32,2,512]{2,1,0:T(2,128)(2,1)S(1)}, u32[]{:S(2)}, u32[]{:S(2)}) async-start(bf16[32,2,512]{2,1,0:T(2,128)(2,1)} %reshape.31), calls=%async_computation.2 | async-start | bytes 131072 | tf_op jit(solution)/shard_map/all_to_all | solution.py:18
  13.7 3.9 %add_convert_fusion.1 = bf16[16,64,768]{2,1,0:T(8,128)(2,1)} fusion(f32[16,64,768]{2,1,0:T(8,128)} %param.6, bf16[16,64,768]{2,1,0:T(8,128)(2,1)} %param.7), kind=kLoop, calls=%fused_computation.1 | loop fusion | flops 2359296 | bytes 6291456 | tf_op jit(solution)/shard_map/convert_element_type | solution.py:57
  17.6 4.0 %copy.48 = bf16[16,64,768]{1,0,2:T(8,128)(2,1)S(1)} copy(bf16[16,64,768]{2,1,0:T(8,128)(2,1)} %add_convert_fusion.1) | data formatting | bytes 3145728 | tf_op jit(solution)/shard_map/convert_element_type | solution.py:57
  21.6 3.2 %reshape.27 = bf16[32,2,12288]{2,1,0:T(2,128)(2,1)} reshape(bf16[768,16,64]{2,1,0:T(8,128)(2,1)S(1)} %bitcast.34) | data formatting | bytes 3145728
  24.8 0.0 copy-start
  24.8 0.0 all-to-all-done.2
  24.8 10.1 %all-to-all-start = ((bf16[32,2,12288]{2,1,0:T(2,128)(2,1)}), bf16[32,2,12288]{2,1,0:T(2,128)(2,1)}, u32[]{:S(2)}, u32[]{:S(2)}) async-start(bf16[32,2,12288]{2,1,0:T(2,128)(2,1)} %reshape.27), calls=%async_computation | async-start | bytes 3145728 | tf_op jit(solution)/shard_map/all_to_all | solution.py:59
  34.9 0.0 copy-done
  34.9 3.0 %add_convert_fusion = bf16[16,64,768]{2,1,0:T(8,128)(2,1)} fusion(f32[16,64,768]{2,1,0:T(8,128)S(1)} %copy-done, bf16[16,64,768]{2,1,0:T(8,128)(2,1)} %param.9), kind=kLoop, calls=%fused_computation | loop fusion | flops 2359296 | bytes 6291456 | tf_op jit(solution)/shard_map/convert_element_type | solution.py:57
  37.9 4.0 %copy.51 = bf16[16,64,768]{1,0,2:T(8,128)(2,1)S(1)} copy(bf16[16,64,768]{2,1,0:T(8,128)(2,1)} %add_convert_fusion) | data formatting | bytes 3145728 | tf_op jit(solution)/shard_map/convert_element_type | solution.py:57
  41.9 3.2 %reshape.29 = bf16[32,2,12288]{2,1,0:T(2,128)(2,1)} reshape(bf16[768,16,64]{2,1,0:T(8,128)(2,1)S(1)} %bitcast.35) | data formatting | bytes 3145728
  45.1 28.6 %all-to-all-done = bf16[32,2,12288]{2,1,0:T(2,128)(2,1)} async-done(((bf16[32,2,12288]{2,1,0:T(2,128)(2,1)}), bf16[32,2,12288]{2,1,0:T(2,128)(2,1)}, u32[]{:S(2)}, u32[]{:S(2)}) %all-to-all-start) | async-done | bytes 1572896 | tf_op jit(solution)/shard_map/all_to_all | solution.py:59
  73.7 5.6 %all-to-all-start.1 = ((bf16[32,2,12288]{2,1,0:T(2,128)(2,1)}), bf16[32,2,12288]{2,1,0:T(2,128)(2,1)}, u32[]{:S(2)}, u32[]{:S(2)}) async-start(bf16[32,2,12288]{2,1,0:T(2,128)(2,1)} %reshape.29), calls=%async_computation.1 | async-start | bytes 3145728 | tf_op jit(solution)/shard_map/all_to_all | solution.py:60
  79.3 0.1 reshape.32
  79.5 0.1 all_gather.28
  79.6 12.7 %all_gather.29 = bf16[4,1024,16]{1,2,0:T(8,128)(2,1)S(1)} all-gather(bf16[1,1024,16]{1,2,0:T(8,128)(2,1)S(1)} %all_gather.28), channel_id=1, replica_groups=mesh['expert_0'=4,'expert_1'=2,'shard'=32] {'expert_0'}, dimensions={0}, use_global_device_ids=true | all-gather | bytes 163840 | tf_op jit(solution)/shard_map/all_gather | solution.py:35
  92.3 2.0 %all-gather.1 = bf16[8,1024,16]{1,2,0:T(8,128)(2,1)S(1)} all-gather(bf16[4,1024,16]{1,2,0:T(8,128)(2,1)S(1)} %all_gather.29), channel_id=3, replica_groups=mesh['expert_0'=4,'expert_1'=2,'shard'=32] {'expert_1'}, dimensions={0}, use_global_device_ids=true | all-gather | bytes 393216 | tf_op jit(solution)/shard_map/all_gather | solution.py:35
  94.3 0.1 all_gather.24
  94.5 1.9 %all_gather.25 = bf16[2,1024,16]{1,2,0:T(8,128)(2,1)S(1)} all-gather(bf16[1,1024,16]{1,2,0:T(8,128)(2,1)S(1)} %all_gather.24), channel_id=1, replica_groups=mesh['expert_0'=4,'expert_1'=2,'shard'=32] {'expert_1'}, dimensions={0}, use_global_device_ids=true | all-gather | bytes 98304 | tf_op jit(solution)/shard_map/all_gather | solution.py:35
  96.3 12.4 %all-gather = bf16[8,1024,16]{1,2,0:T(8,128)(2,1)S(1)} all-gather(bf16[2,1024,16]{1,2,0:T(8,128)(2,1)S(1)} %all_gather.25), channel_id=2, replica_groups=mesh['expert_0'=4,'expert_1'=2,'shard'=32] {'expert_0'}, dimensions={0}, use_global_device_ids=true | all-gather | bytes 327680 | tf_op jit(solution)/shard_map/all_gather | solution.py:35
  108.8 1.0 copy.57
  109.8 5.1 %reshape.28 = bf16[768,16,64]{2,1,0:T(8,128)(2,1)S(1)} reshape(bf16[32,2,12288]{2,1,0:T(2,128)(2,1)} %all-to-all-done) | data formatting | bytes 3145728
  114.9 3.7 %copy.50 = bf16[16,32,64,24]{2,1,3,0:T(8,128)(2,1)} copy(bf16[16,32,64,24]{2,0,3,1:T(8,128)(2,1)S(1)} %bitcast.36) | data formatting | bytes 3145728 | tf_op jit(solution)/shard_map/all_to_all | solution.py:59
  118.6 5.6 %all_to_all.32 = bf16[16,2048,24]{1,2,0:T(8,128)(2,1)} reshape(bf16[16,32,64,24]{2,1,3,0:T(8,128)(2,1)} %copy.50) | data formatting | bytes 3145728 | tf_op jit(solution)/shard_map/all_to_all | solution.py:59
  124.1 0.0 all-to-all-done.1
  124.1 5.1 %reshape.30 = bf16[768,16,64]{2,1,0:T(8,128)(2,1)S(1)} reshape(bf16[32,2,12288]{2,1,0:T(2,128)(2,1)} %all-to-all-done.1) | data formatting | bytes 3145728
  129.2 3.7 %copy.53 = bf16[16,32,64,24]{2,1,3,0:T(8,128)(2,1)} copy(bf16[16,32,64,24]{2,0,3,1:T(8,128)(2,1)S(1)} %bitcast.37) | data formatting | bytes 3145728 | tf_op jit(solution)/shard_map/all_to_all | solution.py:60
  132.9 5.6 %all_to_all.36 = bf16[16,2048,24]{1,2,0:T(8,128)(2,1)} reshape(bf16[16,32,64,24]{2,1,3,0:T(8,128)(2,1)} %copy.53) | data formatting | bytes 3145728 | tf_op jit(solution)/shard_map/all_to_all | solution.py:60
  (6 shorter events, 0.1 us)
Async XLA Ops:
  2.1 22.7 %all-to-all-start.2 = ((bf16[32,2,512]{2,1,0:T(2,128)(2,1)}), bf16[32,2,512]{2,1,0:T(2,128)(2,1)S(1)}, u32[]{:S(2)}, u32[]{:S(2)}) async-start(bf16[32,2,512]{2,1,0:T(2,128)(2,1)} %reshape.31), calls=%async_computation.2 | async-start | bytes 131072 | tf_op jit(solution)/shard_map/all_to_all | solution.py:18
  24.8 10.1 %copy-start = (f32[16,64,768]{2,1,0:T(8,128)S(1)}, f32[16,64,768]{2,1,0:T(8,128)}, u32[]{:S(2)}) copy-start(f32[16,64,768]{2,1,0:T(8,128)} %param.8) | copy-start | bytes 9437188
  24.8 48.9 %all-to-all-start = ((bf16[32,2,12288]{2,1,0:T(2,128)(2,1)}), bf16[32,2,12288]{2,1,0:T(2,128)(2,1)}, u32[]{:S(2)}, u32[]{:S(2)}) async-start(bf16[32,2,12288]{2,1,0:T(2,128)(2,1)} %reshape.27), calls=%async_computation | async-start | bytes 3145728 | tf_op jit(solution)/shard_map/all_to_all | solution.py:59
  73.7 50.4 %all-to-all-start.1 = ((bf16[32,2,12288]{2,1,0:T(2,128)(2,1)}), bf16[32,2,12288]{2,1,0:T(2,128)(2,1)}, u32[]{:S(2)}, u32[]{:S(2)}) async-start(bf16[32,2,12288]{2,1,0:T(2,128)(2,1)} %reshape.29), calls=%async_computation.1 | async-start | bytes 3145728 | tf_op jit(solution)/shard_map/all_to_all | solution.py:60
where the time goes:
time: 139 us; the launch traced here: 138 us
  local copies, waits for them, and re-layouts  45.3 us (33%)
  blocking collectives  28.9 us (21%)
  waiting for transfers between devices  28.6 us (21%)
  starting transfers between devices  27.3 us (20%)
  other arithmetic  7.6 us (5%)
    all_gather x4, blocking collectives, gather_in_order(): parts = lax.all_gather(parts, axes[k])  28.9 us
    all_to_all x1, waiting for transfers between devices, shards(): lax.all_to_all(narrow_gate, 'shard', split_axis=2, concat_axis=1, tiled=T...  28.6 us
    unnamed x10, local copies, waits for them, and re-layouts  18.5 us
    all_to_all x1, starting transfers between devices, copy_for_each(): return lax.all_to_all(copies, axis, split_axis=0, concat_axis=0, tiled=True)  11.6 us
    all_to_all x1, starting transfers between devices, shards(): lax.all_to_all(narrow_gate, 'shard', split_axis=2, concat_axis=1, tiled=T...  10.1 us
    all_to_all x2, local copies, waits for them, and re-layouts, shards(): lax.all_to_all(narrow_gate, 'shard', split_axis=2, concat_axis=1, tiled=T...  9.25 us
    all_to_all x2, local copies, waits for them, and re-layouts, shards(): lax.all_to_all(narrow_up, 'shard', split_axis=2, concat_axis=1, tiled=True)  9.25 us
    all_to_all x1, starting transfers between devices, shards(): lax.all_to_all(narrow_up, 'shard', split_axis=2, concat_axis=1, tiled=True)  5.61 us
  transfers between devices with their start and end apart: 3, of which 1 were waited for; matrix products, arithmetic and copies ran while one was open for 23% of the time, Pallas kernels for 0%

commit v1 on v0

--- a/solution.py
+++ b/solution.py
@@ -5,6 +5,18 @@
 from jax.sharding import PartitionSpec as P
 
 EXPERT = ("expert_0", "expert_1")
+
+
+def handle_the_tables(x0, which_dim, array_dim):
+    return jnp.concatenate(
+        lax.all_to_all(
+            jnp.stack(jnp.split(x0, lax.psum(1, axis_name="shard"), which_dim), 0),
+            axis_name="shard",
+            split_axis=0,
+            concat_axis=0,
+        ),
+        array_dim,
+    )
 
 
 def laid_out(parts, dim):
@@ -56,7 +68,7 @@
     merged_up = master_up + second_up.astype(jnp.float32)
     narrow_gate, narrow_up = (merged_gate.astype(jnp.bfloat16), merged_up.astype(jnp.bfloat16))
     final_gate, final_up = (
-        lax.all_to_all(narrow_gate, "shard", split_axis=2, concat_axis=1, tiled=True),
+        handle_the_tables(narrow_gate, 2, 1),
         lax.all_to_all(narrow_up, "shard", split_axis=2, concat_axis=1, tiled=True),
     )
     final_gate = jnp.transpose(final_gate, (0, 2, 1))

time: 139 us -> 141 us (1.014)
  local copies, waits for them, and re-layouts: 45.3 us -> 47.5 us
    unnamed x10 -> x43, local copies, waits for them, and re-layouts: 18.5 us -> 27.9 us
    all_to_all x2 -> x0, local copies, waits for them, and re-layouts: 9.25 us -> none  [shards(): lax.all_to_all(narrow_gate, 'shard', split_axis=2, concat_axis=1, tiled=T...]
    reshape x0 -> x3, local copies, waits for them, and re-layouts: none -> 5.97 us  [handle_the_tables(): jnp.concatenate(lax.all_to_all(jnp.stack(jnp.split(x0, lax.psum(1, axis_n...]
    convert_element_type x1 -> x0, local copies, waits for them, and re-layouts: 4.02 us -> none  [shards(): merged_gate.astype(jnp.bfloat16)]
  transfers between devices with their start and end apart: 3 -> 3, of which waited for: 1 -> 1; matrix products, arithmetic and copies ran while one was open for 23% -> 28% of each run, Pallas kernels for 0% -> 0%
where the time goes in v1:
time: 141 us
  local copies, waits for them, and re-layouts  47.5 us (34%)
  blocking collectives  28.9 us (20%)
  waiting for transfers between devices  28.6 us (20%)
  starting transfers between devices  27.3 us (19%)
  other arithmetic  7.27 us (5%)
    all_gather x4, blocking collectives, gather_in_order(): parts = lax.all_gather(parts, axes[k])  28.9 us
    all_to_all x1, waiting for transfers between devices, handle_the_tables(): lax.all_to_all(jnp.stack(jnp.split(x0, lax.psum(1, axis_name='shard'), wh...  28.6 us
    unnamed x43, local copies, waits for them, and re-layouts  27.9 us
    all_to_all x1, starting transfers between devices, copy_for_each(): return lax.all_to_all(copies, axis, split_axis=0, concat_axis=0, tiled=True)  11.6 us
    all_to_all x1, starting transfers between devices, handle_the_tables(): lax.all_to_all(jnp.stack(jnp.split(x0, lax.psum(1, axis_name='shard'), wh...  10.1 us
    all_to_all x2, local copies, waits for them, and re-layouts, shards(): lax.all_to_all(narrow_up, 'shard', split_axis=2, concat_axis=1, tiled=True)  9.25 us
    reshape x3, local copies, waits for them, and re-layouts, handle_the_tables(): jnp.concatenate(lax.all_to_all(jnp.stack(jnp.split(x0, lax.psum(1, axis_n...  5.97 us
    all_to_all x1, starting transfers between devices, shards(): lax.all_to_all(narrow_up, 'shard', split_axis=2, concat_axis=1, tiled=True)  5.61 us
  transfers between devices with their start and end apart: 3, of which 1 were waited for; matrix products, arithmetic and copies ran while one was open for 28% of the time, Pallas kernels for 0%

profile of v1, /device:TPU:6, one launch (start us, length us, event | category | flops | bytes accessed | tf_op | source)
XLA Modules:
  0.0 140.6 jit_solution(339826949255030993)
XLA Ops:
  0.6 0.7 multiply_convert_fusion
  1.4 0.8 reshape.39
  2.1 11.6 %all-to-all-start.2 = ((bf16[32,2,512]{2,1,0:T(2,128)(2,1)}), bf16[32,2,512]{2,1,0:T(2,128)(2,1)S(1)}, u32[]{:S(2)}, u32[]{:S(2)}) async-start(bf16[32,2,512]{2,1,0:T(2,128)(2,1)} %reshape.39), calls=%async_computation.2 | async-start | bytes 131072 | tf_op jit(solution)/shard_map/all_to_all | solution.py:30
  13.7 5.8 %copy.43 = f32[16,64,768]{1,2,0:T(8,128)} copy(f32[16,64,768]{2,1,0:T(8,128)} %param.6) | data formatting | bytes 6291456 | tf_op args[0]
  19.5 3.1 %copy.42 = bf16[16,64,768]{1,2,0:T(8,128)(2,1)S(1)} copy(bf16[16,64,768]{2,1,0:T(8,128)(2,1)} %param.7) | data formatting | bytes 3145728 | tf_op args[1]
  22.6 3.6 %add_convert_fusion = bf16[16,64,768]{1,2,0:T(8,128)(2,1)S(1)} fusion(f32[16,64,768]{1,2,0:T(8,128)} %copy.43, bf16[16,64,768]{1,2,0:T(8,128)(2,1)S(1)} %copy.42), kind=kLoop, calls=%fused_computation | loop fusion | flops 2359296 | bytes 6291456 | tf_op jit(solution)/shard_map/convert_element_type | solution.py:69
  27.0 3.2 %reshape.35 = bf16[32,2,12288]{2,1,0:T(2,128)(2,1)} reshape(bf16[32,16,24,64]{3,2,1,0:T(8,128)(2,1)S(1)} %bitcast.164) | data formatting | bytes 3145728
  30.1 0.0 copy-start
  30.1 0.0 all-to-all-done.2
  30.1 10.1 %all-to-all-start = ((bf16[32,2,12288]{2,1,0:T(2,128)(2,1)}), bf16[32,2,12288]{2,1,0:T(2,128)(2,1)}, u32[]{:S(2)}, u32[]{:S(2)}) async-start(bf16[32,2,12288]{2,1,0:T(2,128)(2,1)} %reshape.35), calls=%async_computation | async-start | bytes 3145728 | tf_op jit(solution)/shard_map/all_to_all | solution.py:12
  40.2 0.0 copy-done
  40.2 3.0 %add_convert_fusion.1 = bf16[16,64,768]{2,1,0:T(8,128)(2,1)} fusion(f32[16,64,768]{2,1,0:T(8,128)S(1)} %copy-done, bf16[16,64,768]{2,1,0:T(8,128)(2,1)} %param.9), kind=kLoop, calls=%fused_computation.1 | loop fusion | flops 2359296 | bytes 6291456 | tf_op jit(solution)/shard_map/convert_element_type | solution.py:69
  43.2 4.0 %copy.45 = bf16[16,64,768]{1,0,2:T(8,128)(2,1)S(1)} copy(bf16[16,64,768]{2,1,0:T(8,128)(2,1)} %add_convert_fusion.1) | data formatting | bytes 3145728 | tf_op jit(solution)/shard_map/convert_element_type | solution.py:69
  47.2 3.2 %reshape.37 = bf16[32,2,12288]{2,1,0:T(2,128)(2,1)} reshape(bf16[768,16,64]{2,1,0:T(8,128)(2,1)S(1)} %bitcast.162) | data formatting | bytes 3145728
  50.4 28.6 %all-to-all-done = bf16[32,2,12288]{2,1,0:T(2,128)(2,1)} async-done(((bf16[32,2,12288]{2,1,0:T(2,128)(2,1)}), bf16[32,2,12288]{2,1,0:T(2,128)(2,1)}, u32[]{:S(2)}, u32[]{:S(2)}) %all-to-all-start) | async-done | bytes 1572896 | tf_op jit(solution)/shard_map/all_to_all | solution.py:12
  79.0 5.6 %all-to-all-start.1 = ((bf16[32,2,12288]{2,1,0:T(2,128)(2,1)}), bf16[32,2,12288]{2,1,0:T(2,128)(2,1)}, u32[]{:S(2)}, u32[]{:S(2)}) async-start(bf16[32,2,12288]{2,1,0:T(2,128)(2,1)} %reshape.37), calls=%async_computation.1 | async-start | bytes 3145728 | tf_op jit(solution)/shard_map/all_to_all | solution.py:72
  84.7 0.1 reshape.40
  84.8 0.1 all_gather.28
  85.0 12.7 %all_gather.29 = bf16[4,1024,16]{1,2,0:T(8,128)(2,1)S(1)} all-gather(bf16[1,1024,16]{1,2,0:T(8,128)(2,1)S(1)} %all_gather.28), channel_id=1, replica_groups=mesh['expert_0'=4,'expert_1'=2,'shard'=32] {'expert_0'}, dimensions={0}, use_global_device_ids=true | all-gather | bytes 163840 | tf_op jit(solution)/shard_map/all_gather | solution.py:47
  97.6 2.0 %all-gather.1 = bf16[8,1024,16]{1,2,0:T(8,128)(2,1)S(1)} all-gather(bf16[4,1024,16]{1,2,0:T(8,128)(2,1)S(1)} %all_gather.29), channel_id=3, replica_groups=mesh['expert_0'=4,'expert_1'=2,'shard'=32] {'expert_1'}, dimensions={0}, use_global_device_ids=true | all-gather | bytes 393216 | tf_op jit(solution)/shard_map/all_gather | solution.py:47
  99.7 0.1 all_gather.24
  99.8 1.9 %all_gather.25 = bf16[2,1024,16]{1,2,0:T(8,128)(2,1)S(1)} all-gather(bf16[1,1024,16]{1,2,0:T(8,128)(2,1)S(1)} %all_gather.24), channel_id=1, replica_groups=mesh['expert_0'=4,'expert_1'=2,'shard'=32] {'expert_1'}, dimensions={0}, use_global_device_ids=true | all-gather | bytes 98304 | tf_op jit(solution)/shard_map/all_gather | solution.py:47
  101.6 12.4 %all-gather = bf16[8,1024,16]{1,2,0:T(8,128)(2,1)S(1)} all-gather(bf16[2,1024,16]{1,2,0:T(8,128)(2,1)S(1)} %all_gather.25), channel_id=2, replica_groups=mesh['expert_0'=4,'expert_1'=2,'shard'=32] {'expert_0'}, dimensions={0}, use_global_device_ids=true | all-gather | bytes 327680 | tf_op jit(solution)/shard_map/all_gather | solution.py:47
  114.1 1.0 copy.51
  115.1 5.1 %reshape.36 = bf16[32,16,24,64]{3,2,1,0:T(8,128)(2,1)S(1)} reshape(bf16[32,2,12288]{2,1,0:T(2,128)(2,1)} %all-to-all-done) | data formatting | bytes 3145728
  120.2 0.5 bitcast_bitcast_fusion
  120.8 2.0 %copy.44 = bf16[16,32,64,24]{2,1,3,0:T(8,128)(2,1)S(1)} copy(bf16[16,32,64,24]{2,3,0,1:T(8,128)(2,1)S(1)} %bitcast_bitcast_fusion) | data formatting | bytes 3145728 | tf_op jit(solution)/shard_map/reshape | solution.py:11
  122.8 3.4 %reshape.28 = bf16[16,2048,24]{1,2,0:T(8,128)(2,1)} reshape(bf16[16,32,64,24]{2,1,3,0:T(8,128)(2,1)S(1)} %copy.44) | data formatting | bytes 3145728 | tf_op jit(solution)/shard_map/reshape | solution.py:11
  126.2 0.0 all-to-all-done.1
  126.2 5.1 %reshape.38 = bf16[768,16,64]{2,1,0:T(8,128)(2,1)S(1)} reshape(bf16[32,2,12288]{2,1,0:T(2,128)(2,1)} %all-to-all-done.1) | data formatting | bytes 3145728
  131.3 3.7 %copy.47 = bf16[16,32,64,24]{2,1,3,0:T(8,128)(2,1)} copy(bf16[16,32,64,24]{2,0,3,1:T(8,128)(2,1)S(1)} %bitcast.163) | data formatting | bytes 3145728 | tf_op jit(solution)/shard_map/all_to_all | solution.py:72
  135.0 5.6 %all_to_all.23 = bf16[16,2048,24]{1,2,0:T(8,128)(2,1)} reshape(bf16[16,32,64,24]{2,1,3,0:T(8,128)(2,1)} %copy.47) | data formatting | bytes 3145728 | tf_op jit(solution)/shard_map/all_to_all | solution.py:72
  (38 shorter events, 0.7 us)
Async XLA Ops:
  2.1 28.0 %all-to-all-start.2 = ((bf16[32,2,512]{2,1,0:T(2,128)(2,1)}), bf16[32,2,512]{2,1,0:T(2,128)(2,1)S(1)}, u32[]{:S(2)}, u32[]{:S(2)}) async-start(bf16[32,2,512]{2,1,0:T(2,128)(2,1)} %reshape.39), calls=%async_computation.2 | async-start | bytes 131072 | tf_op jit(solution)/shard_map/all_to_all | solution.py:30
  30.1 10.1 %copy-start = (f32[16,64,768]{2,1,0:T(8,128)S(1)}, f32[16,64,768]{2,1,0:T(8,128)}, u32[]{:S(2)}) copy-start(f32[16,64,768]{2,1,0:T(8,128)} %param.8) | copy-start | bytes 9437188
  30.1 48.9 %all-to-all-start = ((bf16[32,2,12288]{2,1,0:T(2,128)(2,1)}), bf16[32,2,12288]{2,1,0:T(2,128)(2,1)}, u32[]{:S(2)}, u32[]{:S(2)}) async-start(bf16[32,2,12288]{2,1,0:T(2,128)(2,1)} %reshape.35), calls=%async_computation | async-start | bytes 3145728 | tf_op jit(solution)/shard_map/all_to_all | solution.py:12
  79.0 47.2 %all-to-all-start.1 = ((bf16[32,2,12288]{2,1,0:T(2,128)(2,1)}), bf16[32,2,12288]{2,1,0:T(2,128)(2,1)}, u32[]{:S(2)}, u32[]{:S(2)}) async-start(bf16[32,2,12288]{2,1,0:T(2,128)(2,1)} %reshape.37), calls=%async_computation.1 | async-start | bytes 3145728 | tf_op jit(solution)/shard_map/all_to_all | solution.py:72
